TPU v7x, 32 devices: a whole 2x2x4 slice. The times are simulated.
32 devices in a mesh: dp: 8 (over z, y), tensor: 4 (over x, core).
Axes of the slice: x: 2, y: 2, z: 4, core: 2. Of those that a mesh axis runs over, the one named last changes fastest.
Arguments:
- tokens: bfloat16 [1024, 16, 768], P(('dp', 'tensor')), may hold values from -6 to 6
- lengths: int32 [16], replicated, may hold values from 1 to 1024, 12288 in all
- dealing: int32 [16], replicated, may hold values from 0 to 15, each once
- project_weight: bfloat16 [768, 2304], P('dp', 'tensor'), may hold values from -0.21875 to 0.21875
- query_projection_bias: float32 [768], replicated, may hold values from -3 to 3
- value_projection_bias: float32 [768], replicated, may hold values from -3 to 3
- attention_output_weight: bfloat16 [768, 768], P('dp', 'tensor'), may hold values from -3.5 to 3.5
- attention_output_bias: float32 [768], replicated, may hold values from -3 to 3
- first_gain: float32 [768], replicated, may hold values from 0.5 to 1.5
- first_shift: float32 [768], replicated, may hold values from -3 to 3
- feed_input_weight: bfloat16 [768, 3072], P('dp', 'tensor'), may hold values from -0.21875 to 0.21875
- feed_input_bias: float32 [3072], replicated, may hold values from -3 to 3
- feed_output_weight: bfloat16 [768, 3072], P('dp', 'tensor'), may hold values from -0.109375 to 0.109375
- feed_output_bias: float32 [768], replicated, may hold values from -3 to 3
- second_gain: float32 [768], replicated, may hold values from 0.5 to 1.5
- second_shift: float32 [768], replicated, may hold values from -3 to 3
- output_grad: bfloat16 [1024, 16, 768], P(('dp', 'tensor')), may hold values from -6 to 6
Outputs:
- layer_output: bfloat16 [1024, 16, 768], P('tensor', 'dp')
- tokens_grad: bfloat16 [1024, 16, 768], P(('dp', 'tensor'))
- project_grad: float32 [768, 2304], P('dp', 'tensor')
- query_bias_grad: float32 [768], P(('dp', 'tensor'))
- value_bias_grad: float32 [768], P(('dp', 'tensor'))
- output_weight_grad: float32 [768, 768], P('dp', 'tensor')
- output_bias_grad: float32 [768], P(('dp', 'tensor'))
- first_gain_grad: float32 [768], P(('dp', 'tensor'))
- first_shift_grad: float32 [768], P(('dp', 'tensor'))
- up_weight_grad: float32 [768, 3072], P('dp', 'tensor')
- up_bias_grad: float32 [3072], P(('dp', 'tensor'))
- down_weight_grad: float32 [768, 3072], P('dp', 'tensor')
- down_bias_grad: float32 [768], P(('dp', 'tensor'))
- second_gain_grad: float32 [768], P(('dp', 'tensor'))
- second_shift_grad: float32 [768], P(('dp', 'tensor'))
Inputs may be any that keep to these rules, and one draw needn't show every extreme that they name: `lengths`: the longest sequence has exactly 1024 tokens. A permutation: sequence s is processed in slot dealing[s], and slot q belongs to data index q // 2.
All inputs are finite; a program needn't handle non-finite values.
Results may differ from a plain program's by a relative error of at most 0.022.
Values may be sent and summed in bfloat16 or wider, within the bound.
A program may use at most 128 MiB of HBM per device.

v0:
```python
from functools import partial
import jax
import jax.numpy as jnp
from jax import lax
from jax.sharding import PartitionSpec as P

HD = 64
EPSILON = 1e-12
MASKED = -1e30


def norm_forward(value, gain, shift):
    centred = value - jnp.mean(value, axis=-1, keepdims=True)
    inverse = lax.rsqrt(jnp.mean(centred * centred, axis=-1, keepdims=True) + EPSILON)
    normed = centred * inverse
    return (normed * gain + shift, normed, inverse)


def norm_backward(upstream, normed, inverse, gain):
    scaled = upstream * gain
    first_mean = jnp.mean(scaled, axis=-1, keepdims=True)
    second_mean = jnp.mean(scaled * normed, axis=-1, keepdims=True)
    return inverse * (scaled - first_mean - normed * second_mean)


def spread_block(values, block_index, length_total):
    blank = jnp.zeros((length_total,), jnp.float32)
    return lax.dynamic_update_slice_in_dim(blank, values, block_index * values.shape[0], 0)


def gather_rows(block):
    return lax.all_gather(block, "tensor", axis=0, tiled=True)


def scatter_rows(partial_sum):
    return lax.psum_scatter(
        partial_sum.astype(jnp.bfloat16), "tensor", scatter_dimension=0, tiled=True
    ).astype(jnp.float32)


def scatter_weight(grad):
    return lax.psum_scatter(
        grad.astype(jnp.bfloat16), "dp", scatter_dimension=0, tiled=True
    ).astype(jnp.float32)


def on_device(
    tokens,
    lengths,
    dealing,
    project_weight,
    query_projection_bias,
    value_projection_bias,
    attention_output_weight,
    attention_output_bias,
    first_gain,
    first_shift,
    feed_input_weight,
    feed_input_bias,
    feed_output_weight,
    feed_output_bias,
    second_gain,
    second_shift,
    output_grad,
):
    n_data = lax.axis_size("dp")
    n_tensor = lax.axis_size("tensor")
    n_all = n_data * n_tensor
    data_index = lax.axis_index("dp")
    tensor_index = lax.axis_index("tensor")
    seq_total = dealing.shape[0]
    seq_here = seq_total // n_data
    piece_rows = tokens.shape[0]
    local_rows = piece_rows * n_data
    seq_rows = local_rows * n_tensor
    width = tokens.shape[2]
    head_cols = attention_output_weight.shape[1]
    heads_here = head_cols // HD
    hidden_cols = feed_input_weight.shape[1]
    score_scale = HD ** (-0.5)
    slot_ids = jnp.arange(seq_total, dtype=jnp.int32)
    placing = (dealing[None, :] == slot_ids[:, None]).astype(jnp.bfloat16)
    send_tokens = jnp.einsum(
        "qs,psd->pqd", placing, tokens, preferred_element_type=jnp.float32
    ).astype(jnp.bfloat16)
    send_grad = jnp.einsum(
        "qs,psd->pqd", placing, output_grad, preferred_element_type=jnp.float32
    ).astype(jnp.bfloat16)
    tokens_here = lax.all_to_all(send_tokens, "dp", split_axis=1, concat_axis=0, tiled=True)
    cotangent_here = lax.all_to_all(send_grad, "dp", split_axis=1, concat_axis=0, tiled=True)
    my_slots = data_index * seq_here + jnp.arange(seq_here, dtype=jnp.int32)
    mine = dealing[None, :] == my_slots[:, None]
    seq_length = jnp.sum(jnp.where(mine, lengths[None, :], 0), axis=1)
    row_ids = jnp.arange(seq_rows, dtype=jnp.int32)
    owner_rows = row_ids // local_rows
    inner_rows = row_ids % local_rows
    position = (
        inner_rows // piece_rows * n_tensor + owner_rows
    ) * piece_rows + inner_rows % piece_rows
    key_valid = position[None, :] < seq_length[:, None]
    project_full = lax.all_gather(project_weight, "dp", axis=0, tiled=True)
    output_full = lax.all_gather(attention_output_weight, "dp", axis=0, tiled=True)
    up_full = lax.all_gather(feed_input_weight, "dp", axis=0, tiled=True)
    down_full = lax.all_gather(feed_output_weight, "dp", axis=0, tiled=True)
    query_part = lax.dynamic_slice_in_dim(
        query_projection_bias, tensor_index * head_cols, head_cols
    )
    value_part = lax.dynamic_slice_in_dim(
        value_projection_bias, tensor_index * head_cols, head_cols
    )
    project_bias = jnp.concatenate([query_part, jnp.zeros_like(query_part), value_part])
    up_bias_here = lax.dynamic_slice_in_dim(
        feed_input_bias, tensor_index * hidden_cols, hidden_cols
    )

    def split_heads(qkv_block):
        query_rows = qkv_block[:, :head_cols].reshape(seq_rows, heads_here, HD)
        key_rows = qkv_block[:, head_cols : 2 * head_cols].reshape(seq_rows, heads_here, HD)
        value_rows = qkv_block[:, 2 * head_cols :].reshape(seq_rows, heads_here, HD)
        return (query_rows, key_rows, value_rows)

    def masked_scores(query_rows, key_rows, valid_keys):
        raw_scores = (
            jnp.einsum("qhe,khe->hqk", query_rows, key_rows, preferred_element_type=jnp.float32)
            * score_scale
        )
        return jnp.where(valid_keys[None, None, :], raw_scores, MASKED)

    def attend(qkv_block, valid_keys):
        query_rows, key_rows, value_rows = split_heads(qkv_block)
        scores = masked_scores(query_rows, key_rows, valid_keys)
        row_max = jnp.max(scores, axis=-1, keepdims=True)
        exponent = jnp.exp(scores - row_max)
        row_total = jnp.sum(exponent, axis=-1, keepdims=True)
        weights = (exponent / row_total).astype(jnp.bfloat16)
        mixed_heads = jnp.einsum(
            "hqk,khe->qhe", weights, value_rows, preferred_element_type=jnp.float32
        )
        return (
            mixed_heads.reshape(seq_rows, head_cols).astype(jnp.bfloat16),
            (row_max + jnp.log(row_total))[..., 0],
        )

    def attend_back(qkv_block, valid_keys, row_lse, grad_block):
        query_rows, key_rows, value_rows = split_heads(qkv_block)
        weights = jnp.exp(masked_scores(query_rows, key_rows, valid_keys) - row_lse[..., None])
        grad_heads = grad_block.reshape(seq_rows, heads_here, HD)
        grad_weights = jnp.einsum(
            "qhe,khe->hqk", grad_heads, value_rows, preferred_element_type=jnp.float32
        )
        inner_sum = jnp.sum(weights * grad_weights, axis=-1, keepdims=True)
        grad_scores = (weights * (grad_weights - inner_sum)).astype(jnp.bfloat16)
        grad_query = (
            jnp.einsum("hqk,khe->qhe", grad_scores, key_rows, preferred_element_type=jnp.float32)
            * score_scale
        )
        grad_key = (
            jnp.einsum("hqk,qhe->khe", grad_scores, query_rows, preferred_element_type=jnp.float32)
            * score_scale
        )
        grad_value = jnp.einsum(
            "hqk,qhe->khe",
            weights.astype(jnp.bfloat16),
            grad_heads,
            preferred_element_type=jnp.float32,
        )
        joined = jnp.concatenate(
            [
                grad_query.reshape(seq_rows, head_cols),
                grad_key.reshape(seq_rows, head_cols),
                grad_value.reshape(seq_rows, head_cols),
            ],
            axis=-1,
        )
        return joined.astype(jnp.bfloat16)

    gelu_exact = partial(jax.nn.gelu, approximate=False)
    seqs = range(seq_here)
    inputs_full = [gather_rows(tokens_here[:, s, :]) for s in seqs]
    projected = [
        (
            jnp.dot(inputs_full[s], project_full, preferred_element_type=jnp.float32) + project_bias
        ).astype(jnp.bfloat16)
        for s in seqs
    ]
    attended = [attend(projected[s], key_valid[s]) for s in seqs]
    mixed = [a[0] for a in attended]
    log_total = [a[1] for a in attended]
    branch = [
        scatter_rows(
            lax.dot_general(
                mixed[s], output_full, (((1,), (1,)), ((), ())), preferred_element_type=jnp.float32
            )
        )
        for s in seqs
    ]
    first = [
        norm_forward(
            tokens_here[:, s, :].astype(jnp.float32) + branch[s] + attention_output_bias,
            first_gain,
            first_shift,
        )
        for s in seqs
    ]
    first_full = [gather_rows(first[s][0].astype(jnp.bfloat16)) for s in seqs]
    preact = [
        jnp.dot(first_full[s], up_full, preferred_element_type=jnp.float32) + up_bias_here
        for s in seqs
    ]
    gelu_pairs = [jax.vjp(gelu_exact, preact[s]) for s in seqs]
    hidden = [g[0].astype(jnp.bfloat16) for g in gelu_pairs]
    feed = [
        scatter_rows(
            lax.dot_general(
                hidden[s], down_full, (((1,), (1,)), ((), ())), preferred_element_type=jnp.float32
            )
        )
        for s in seqs
    ]
    second = [
        norm_forward(first[s][0] + feed[s] + feed_output_bias, second_gain, second_shift)
        for s in seqs
    ]
    layer_output = jnp.stack([second[s][0] for s in seqs], axis=1).astype(jnp.bfloat16)
    cot = [cotangent_here[:, s, :].astype(jnp.float32) for s in seqs]
    second_gain_part = sum((jnp.sum(cot[s] * second[s][1], axis=0) for s in seqs))
    second_shift_part = sum((jnp.sum(cot[s], axis=0) for s in seqs))
    grad_second = [norm_backward(cot[s], second[s][1], second[s][2], second_gain) for s in seqs]
    down_bias_part = sum((jnp.sum(grad_second[s], axis=0) for s in seqs))
    grad_feed_full = [gather_rows(grad_second[s].astype(jnp.bfloat16)) for s in seqs]
    grad_hidden = [
        jnp.dot(grad_feed_full[s], down_full, preferred_element_type=jnp.float32) for s in seqs
    ]
    down_grad = sum(
        (
            lax.dot_general(
                grad_feed_full[s],
                hidden[s],
                (((0,), (0,)), ((), ())),
                preferred_element_type=jnp.float32,
            )
            for s in seqs
        )
    )
    down_shard = scatter_weight(down_grad)
    grad_preact = [gelu_pairs[s][1](grad_hidden[s])[0].astype(jnp.bfloat16) for s in seqs]
    up_grad = sum(
        (
            lax.dot_general(
                first_full[s],
                grad_preact[s],
                (((0,), (0,)), ((), ())),
                preferred_element_type=jnp.float32,
            )
            for s in seqs
        )
    )
    up_shard = scatter_weight(up_grad)
    up_bias_part = sum((jnp.sum(grad_preact[s], axis=0, dtype=jnp.float32) for s in seqs))
    grad_first = [
        grad_second[s]
        + scatter_rows(
            lax.dot_general(
                grad_preact[s],
                up_full,
                (((1,), (1,)), ((), ())),
                preferred_element_type=jnp.float32,
            )
        )
        for s in seqs
    ]
    first_gain_part = sum((jnp.sum(grad_first[s] * first[s][1], axis=0) for s in seqs))
    first_shift_part = sum((jnp.sum(grad_first[s], axis=0) for s in seqs))
    grad_residual = [
        norm_backward(grad_first[s], first[s][1], first[s][2], first_gain) for s in seqs
    ]
    output_bias_part = sum((jnp.sum(grad_residual[s], axis=0) for s in seqs))
    early_vectors = jnp.concatenate(
        [
            v.reshape(n_all, -1)
            for v in (
                output_bias_part,
                first_gain_part,
                first_shift_part,
                spread_block(up_bias_part, tensor_index, hidden_cols * n_tensor),
                down_bias_part,
                second_gain_part,
                second_shift_part,
            )
        ],
        axis=1,
    )
    early_reduced = lax.psum_scatter(
        early_vectors, ("dp", "tensor"), scatter_dimension=0, tiled=True
    )[0]
    branch_grad_full = [gather_rows(grad_residual[s].astype(jnp.bfloat16)) for s in seqs]
    grad_mixed = [
        jnp.dot(branch_grad_full[s], output_full, preferred_element_type=jnp.float32).astype(
            jnp.bfloat16
        )
        for s in seqs
    ]
    output_grad_weight = sum(
        (
            lax.dot_general(
                branch_grad_full[s],
                mixed[s],
                (((0,), (0,)), ((), ())),
                preferred_element_type=jnp.float32,
            )
            for s in seqs
        )
    )
    output_shard = scatter_weight(output_grad_weight)
    grad_projected = [
        attend_back(projected[s], key_valid[s], log_total[s], grad_mixed[s]) for s in seqs
    ]
    project_grad = sum(
        (
            lax.dot_general(
                inputs_full[s],
                grad_projected[s],
                (((0,), (0,)), ((), ())),
                preferred_element_type=jnp.float32,
            )
            for s in seqs
        )
    )
    project_shard = scatter_weight(project_grad)
    bias_sums = sum((jnp.sum(grad_projected[s], axis=0, dtype=jnp.float32) for s in seqs))
    late_vectors = jnp.concatenate(
        [
            spread_block(bias_sums[:head_cols], tensor_index, width).reshape(n_all, -1),
            spread_block(bias_sums[2 * head_cols :], tensor_index, width).reshape(n_all, -1),
        ],
        axis=1,
    )
    late_reduced = lax.psum_scatter(
        late_vectors, ("dp", "tensor"), scatter_dimension=0, tiled=True
    )[0]
    grad_inputs = [
        grad_residual[s]
        + scatter_rows(
            lax.dot_general(
                grad_projected[s],
                project_full,
                (((1,), (1,)), ((), ())),
                preferred_element_type=jnp.float32,
            )
        )
        for s in seqs
    ]
    grad_here = jnp.stack(grad_inputs, axis=1).astype(jnp.bfloat16)
    returned = lax.all_to_all(grad_here, "dp", split_axis=0, concat_axis=1, tiled=True)
    tokens_grad = jnp.einsum(
        "qs,pqd->psd", placing, returned, preferred_element_type=jnp.float32
    ).astype(jnp.bfloat16)
    vec_block = width // n_all
    early_split = [vec_block] * 3 + [hidden_cols * n_tensor // n_all] + [vec_block] * 3
    offsets = [sum(early_split[:k]) for k in range(len(early_split) + 1)]
    early = [early_reduced[offsets[k] : offsets[k + 1]] for k in range(len(early_split))]
    late = [late_reduced[:vec_block], late_reduced[vec_block:]]
    return (
        layer_output,
        tokens_grad,
        project_shard,
        late[0],
        late[1],
        output_shard,
        early[0],
        early[1],
        early[2],
        up_shard,
        early[3],
        down_shard,
        early[4],
        early[5],
        early[6],
    )


def solution(mesh):
    in_specs = (
        P(("dp", "tensor"), None, None),
        P(),
        P(),
        P("dp", "tensor"),
        P(),
        P(),
        P("dp", "tensor"),
        P(),
        P(),
        P(),
        P("dp", "tensor"),
        P(),
        P("dp", "tensor"),
        P(),
        P(),
        P(),
        P(("dp", "tensor"), None, None),
    )
    out_specs = (
        P("tensor", "dp", None),
        P(("dp", "tensor"), None, None),
        P("dp", "tensor"),
        P(("dp", "tensor")),
        P(("dp", "tensor")),
        P("dp", "tensor"),
        P(("dp", "tensor")),
        P(("dp", "tensor")),
        P(("dp", "tensor")),
        P("dp", "tensor"),
        P(("dp", "tensor")),
        P("dp", "tensor"),
        P(("dp", "tensor")),
        P(("dp", "tensor")),
        P(("dp", "tensor")),
    )
    return jax.shard_map(
        on_device, mesh=mesh, in_specs=in_specs, out_specs=out_specs, check_vma=False
    )
```

profile of v0, /device:TPU:0, one launch (start us, length us, event | category | flops | bytes accessed | tf_op | source)
XLA Modules:
  0.0 850.2 jit_solution(14724456239618128440)
XLA Ops:
  10.6 27.4 %all_to_all.54 = bf16[32,16,768]{2,0,1:T(8,128)(2,1)S(1)} all-to-all(bf16[32,16,768]{2,0,1:T(8,128)(2,1)S(1)} %copy.78), channel_id=1, replica_groups=mesh['dp'=8,'tensor'=4] {'dp'}, dimensions={1} | all-to-all | bytes 1572864 | tf_op jit(solution)/shard_map/all_to_all | solution.py:89
  41.7 31.2 %all_gather.38 = bf16[768,192]{1,0:T(8,128)(2,1)S(1)} all-gather(bf16[96,192]{1,0:T(8,128)(2,1)S(1)} %copy-done.49), channel_id=1, replica_groups=mesh['dp'=8,'tensor'=4] {'dp'}, dimensions={0}, use_global_device_ids=true | all-gather | bytes 331776 | tf_op jit(solution)/shard_map/all_gather | solution.py:102
  72.9 32.5 %all_gather.37 = bf16[768,576]{1,0:T(8,128)(2,1)S(1)} all-gather(bf16[96,576]{1,0:T(8,128)(2,1)S(1)} %copy-done.45), channel_id=1, replica_groups=mesh['dp'=8,'tensor'=4] {'dp'}, dimensions={0}, use_global_device_ids=true | all-gather | bytes 995328 | tf_op jit(solution)/shard_map/all_gather | solution.py:101
  136.4 14.9 %reduce-scatter.13.cloned.1.call-done = bf16[256,768]{1,0:T(8,128)(2,1)} async-done(((bf16[1024,768]{1,0:T(8,128)(2,1)}), bf16[256,768]{1,0:T(8,128)(2,1)}) %reduce-scatter.13.cloned.1.call-update) | async-done | bytes 393232 | tf_op jit(solution)/shard_map/reduce_scatter | solution.py:36
  152.6 29.1 %reduce-scatter.17.cloned.1.call-done = bf16[256,768]{1,0:T(8,128)(2,1)} async-done(((bf16[1024,768]{1,0:T(8,128)(2,1)}), bf16[256,768]{1,0:T(8,128)(2,1)}) %reduce-scatter.17.cloned.1.call-update) | async-done | bytes 393232 | tf_op jit(solution)/shard_map/reduce_scatter | solution.py:36
  189.2 17.3 %all-gather.19.cloned.1.call-done = bf16[1024,768]{1,0:T(8,128)(2,1)} async-done(((bf16[256,768]{1,0:T(8,128)(2,1)}), bf16[1024,768]{1,0:T(8,128)(2,1)}) %all-gather.19.cloned.1.call-update) | async-done | bytes 1572880 | tf_op jit(solution)/shard_map/all_gather | solution.py:32
  206.5 4.9 fusion.119
  211.4 16.7 %all-gather.13.cloned.1.call-done = bf16[1024,768]{1,0:T(8,128)(2,1)} async-done(((bf16[256,768]{1,0:T(8,128)(2,1)}), bf16[1024,768]{1,0:T(8,128)(2,1)}) %all-gather.13.cloned.1.call-update) | async-done | bytes 1572880 | tf_op jit(solution)/shard_map/all_gather | solution.py:32
  228.1 17.3 %multiply_convert_fusion.3 = (bf16[1024,768]{1,0:T(8,128)(2,1)}, f32[1024,768]{1,0:T(8,128)}, bf16[1024,768]{1,0:T(8,128)(2,1)}, f32[1024,768]{1,0:T(8,128)}, f32[1024,768]{1,0:T(8,128)}) fusion(f32[768]{0:T(1024)S(1)} %dynamic_slice.11, f32[1024,768]{1,0:T(8,128)} %fusion.119, bf16[1024,768]{1,0:T(8,128)(2,1)} %all-gather.13.cloned.1.call-done, ...), kind=kOutput, calls=%fused_computation.43 | convolution fusion | flops 1311768576 | bytes 18484224 | tf_op jit(solution)/shard_map/dot_general | solution.py:207
  245.4 26.3 %all-gather.17.cloned.1.call-done = bf16[768,768]{1,0:T(8,128)(2,1)} async-done(((bf16[96,768]{1,0:T(8,128)(2,1)}), bf16[768,768]{1,0:T(8,128)(2,1)}) %all-gather.17.cloned.1.call-update) | async-done | bytes 1179664 | tf_op jit(solution)/shard_map/all_gather | solution.py:104
  276.1 4.4 convolution_convert_fusion.4
  282.0 21.2 %all_to_all.55 = bf16[32,16,768]{2,0,1:T(8,128)(2,1)S(1)} all-to-all(bf16[32,16,768]{2,0,1:T(8,128)(2,1)S(1)} %copy.83), channel_id=1, replica_groups=mesh['dp'=8,'tensor'=4] {'dp'}, dimensions={1} | all-to-all | bytes 1572864 | tf_op jit(solution)/shard_map/all_to_all | solution.py:90
  303.4 29.6 %reduce-scatter.19.cloned.1.call-done = bf16[256,768]{1,0:T(8,128)(2,1)} async-done(((bf16[1024,768]{1,0:T(8,128)(2,1)}), bf16[256,768]{1,0:T(8,128)(2,1)}) %reduce-scatter.19.cloned.1.call-update) | async-done | bytes 393232 | tf_op jit(solution)/shard_map/reduce_scatter | solution.py:36
  341.0 18.6 %all-gather.21.cloned.1.call-done = bf16[1024,768]{1,0:T(8,128)(2,1)} async-done(((bf16[256,768]{1,0:T(8,128)(2,1)}), bf16[1024,768]{1,0:T(8,128)(2,1)}) %all-gather.21.cloned.1.call-update) | async-done | bytes 1572880 | tf_op jit(solution)/shard_map/all_gather | solution.py:32
  359.7 4.8 fusion.120
  364.4 16.3 %all-gather.25.cloned.1.call-done = bf16[1024,768]{1,0:T(8,128)(2,1)} async-done(((bf16[256,768]{1,0:T(8,128)(2,1)}), bf16[1024,768]{1,0:T(8,128)(2,1)}) %all-gather.25.cloned.1.call-update) | async-done | bytes 1572880 | tf_op jit(solution)/shard_map/all_gather | solution.py:32
  380.8 11.5 %convert_reduce_fusion = (f32[768]{0:T(1024)}, bf16[1024,768]{1,0:T(8,128)(2,1)}, f32[768]{0:T(1024)}, bf16[1024,768]{1,0:T(8,128)(2,1)S(1)}) fusion(f32[1024,768]{1,0:T(8,128)} %get-tuple-element.152, f32[1024,768]{1,0:T(8,128)} %fusion.119, f32[768]{0:T(1024)} %copy-done.58, f32[1024,768]{1,0:T(8,128)} %fusion.120, f32[1024,768]{1,0:T(8,128)} %get-tuple-element.119, ...), kind=kOutput, calls=%fused_computation.26 | convolution fusion | flops 1234696704 | bytes 21636096 | tf_op jit(solution)/shard_map/dot_general | solution.py:232
  400.6 23.6 %reduce-scatter.21.cloned.1.call-done = bf16[256,768]{1,0:T(8,128)(2,1)} async-done(((bf16[1024,768]{1,0:T(8,128)(2,1)}), bf16[256,768]{1,0:T(8,128)(2,1)}) %reduce-scatter.21.cloned.1.call-update) | async-done | bytes 393232 | tf_op jit(solution)/shard_map/reduce_scatter | solution.py:36
  424.1 30.4 %reduce-scatter.25.cloned.1.call-done = bf16[256,768]{1,0:T(8,128)(2,1)} async-done(((bf16[1024,768]{1,0:T(8,128)(2,1)}), bf16[256,768]{1,0:T(8,128)(2,1)}) %reduce-scatter.25.cloned.1.call-update) | async-done | bytes 393232 | tf_op jit(solution)/shard_map/reduce_scatter | solution.py:36
  466.3 15.8 %all-gather.27.cloned.1.call-done = bf16[1024,768]{1,0:T(8,128)(2,1)} async-done(((bf16[256,768]{1,0:T(8,128)(2,1)}), bf16[1024,768]{1,0:T(8,128)(2,1)}) %all-gather.27.cloned.1.call-update) | async-done | bytes 1572880 | tf_op jit(solution)/shard_map/all_gather | solution.py:32
  484.3 6.1 multiply_reduce_fusion
  493.0 5.2 multiply_convert_fusion
  498.3 5.0 fusion.38
  511.7 6.4 multiply_reduce_fusion.1
  520.7 5.2 multiply_convert_fusion.1
  525.9 5.0 fusion.36
  571.8 5.5 all-to-all-start.2
  578.2 62.9 %reduce-scatter.35.cloned.1.call-done = bf16[96,768]{1,0:T(8,128)(2,1)} async-done(((bf16[768,768]{1,0:T(8,128)(2,1)}), bf16[96,768]{1,0:T(8,128)(2,1)}) %reduce-scatter.35.cloned.1.call-update) | async-done | bytes 147472 | tf_op jit(solution)/shard_map/reduce_scatter | solution.py:42
  642.7 65.5 %reduce-scatter.33.cloned.1.call-done = bf16[96,768]{1,0:T(8,128)(2,1)} async-done(((bf16[768,768]{1,0:T(8,128)(2,1)}), bf16[96,768]{1,0:T(8,128)(2,1)}) %reduce-scatter.33.cloned.1.call-update) | async-done | bytes 147472 | tf_op jit(solution)/shard_map/reduce_scatter | solution.py:42
  716.4 40.2 %all-reduce.2 = (f32[32,48]{1,0:T(8,128)S(1)}, f32[32,240]{1,0:T(8,128)S(1)}) all-reduce(f32[32,48]{1,0:T(8,128)S(1)} %pad_maximum_fusion.4, f32[32,240]{1,0:T(8,128)} %concatenate.21), channel_id=13, replica_groups=mesh['dp'=8,'tensor'=4] {'dp','tensor'}, use_global_device_ids=true, to_apply=%region_34.35.clone | all-reduce | flops 9216 | bytes 73728
  758.5 14.3 %reduce-scatter.31.cloned.1.call-done = bf16[96,192]{1,0:T(8,128)(2,1)} async-done(((bf16[768,192]{1,0:T(8,128)(2,1)}), bf16[96,192]{1,0:T(8,128)(2,1)}) %reduce-scatter.31.cloned.1.call-update) | async-done | bytes 36880 | tf_op jit(solution)/shard_map/reduce_scatter | solution.py:42
  774.2 64.8 %reduce-scatter.29.cloned.1.call-done = bf16[96,576]{1,0:T(8,128)(2,1)} async-done(((bf16[768,576]{1,0:T(8,128)(2,1)}), bf16[96,576]{1,0:T(8,128)(2,1)}) %reduce-scatter.29.cloned.1.call-update) | async-done | bytes 110608 | tf_op jit(solution)/shard_map/reduce_scatter | solution.py:42
  (325 shorter events, 153.0 us)
Async XLA Ops:
  8.0 97.4 %all-gather.31.cloned.1.call-start = ((), (), s32[]{:S(2)}) async-start(), calls=%async_computation.36 | async-start | bytes 1966080 | tf_op jit(solution)/shard_map/all_gather | solution.py:32
  10.6 62.3 %copy-start.45 = (bf16[96,576]{1,0:T(8,128)(2,1)S(1)}, bf16[96,576]{1,0:T(8,128)(2,1)}, u32[]{:S(2)}) copy-start(bf16[96,576]{1,0:T(8,128)(2,1)} %param.20) | copy-start | bytes 331780
  39.0 70.1 %all-gather.29.cloned.1.call-start = ((), (), s32[]{:S(2)}) async-start(), calls=%async_computation.35 | async-start | bytes 1966080 | tf_op jit(solution)/shard_map/all_gather | solution.py:32
  39.7 111.6 %reduce-scatter.13.cloned.1.call-start = ((), (), s32[]{:S(2)}) async-start(), calls=%async_computation.15 | async-start | bytes 1966080 | tf_op jit(solution)/shard_map/reduce_scatter | solution.py:36
  123.7 58.0 %reduce-scatter.17.cloned.1.call-start = ((), (), s32[]{:S(2)}) async-start(), calls=%async_computation.20 | async-start | bytes 1966080 | tf_op jit(solution)/shard_map/reduce_scatter | solution.py:36
  133.9 49.3 %copy-start.25 = (bf16[3,64,1024]{2,1,0:T(8,128)(2,1)}, bf16[3,64,1024]{2,1,0:T(8,128)(2,1)S(1)}, u32[]{:S(2)}) copy-start(bf16[3,64,1024]{2,1,0:T(8,128)(2,1)S(1)} %fusion.46) | copy-start | bytes 1179652
  133.9 50.6 %copy-start.48 = (f32[768]{0:T(1024)S(1)}, f32[768]{0:T(1024)}, u32[]{:S(2)}) copy-start(f32[768]{0:T(1024)} %param.25) | copy-start | bytes 9220
  133.9 50.6 %copy-start.54 = (f32[768]{0:T(1024)S(1)}, f32[768]{0:T(1024)}, u32[]{:S(2)}) copy-start(f32[768]{0:T(1024)} %param.26) | copy-start | bytes 9220
  135.7 53.5 %all-gather.15.cloned.1.call-start = ((), (), s32[]{:S(2)}) async-start(), calls=%async_computation.17 | async-start | bytes 1327104 | tf_op jit(solution)/shard_map/all_gather | solution.py:103
  136.3 70.2 %all-gather.19.cloned.1.call-start = ((), (), s32[]{:S(2)}) async-start(), calls=%async_computation.21 | async-start | bytes 1966080 | tf_op jit(solution)/shard_map/all_gather | solution.py:32
  186.9 41.2 %all-gather.13.cloned.1.call-start = ((), (), s32[]{:S(2)}) async-start(), calls=%async_computation.16 | async-start | bytes 1966080 | tf_op jit(solution)/shard_map/all_gather | solution.py:32
  187.5 84.2 %all-gather.17.cloned.1.call-start = ((), (), s32[]{:S(2)}) async-start(), calls=%async_computation.18 | async-start | bytes 1327104 | tf_op jit(solution)/shard_map/all_gather | solution.py:104
  188.2 115.2 %reduce-scatter.15.cloned.1.call-start = ((), (), s32[]{:S(2)}) async-start(), calls=%async_computation.19 | async-start | bytes 1966080 | tf_op jit(solution)/shard_map/reduce_scatter | solution.py:36
  276.0 57.0 %reduce-scatter.19.cloned.1.call-start = ((), (), s32[]{:S(2)}) async-start(), calls=%async_computation.22 | async-start | bytes 1966080 | tf_op jit(solution)/shard_map/reduce_scatter | solution.py:36
  280.5 52.5 %copy-start.7 = (bf16[256,768]{1,0:T(8,128)(2,1)S(1)}, bf16[256,768]{1,0:T(8,128)(2,1)}, u32[]{:S(2)}) copy-start(bf16[256,768]{1,0:T(8,128)(2,1)} %reduce-scatter.17.cloned.1.call-done) | copy-start | bytes 1179652
  280.5 79.1 %all-gather.21.cloned.1.call-start = ((), (), s32[]{:S(2)}) async-start(), calls=%async_computation.23 | async-start | bytes 1966080 | tf_op jit(solution)/shard_map/all_gather | solution.py:32
  339.9 40.9 %all-gather.25.cloned.1.call-start = ((), (), s32[]{:S(2)}) async-start(), calls=%async_computation.27 | async-start | bytes 1966080 | tf_op jit(solution)/shard_map/all_gather | solution.py:32
  340.8 83.4 %reduce-scatter.21.cloned.1.call-start = ((), (), s32[]{:S(2)}) async-start(), calls=%async_computation.24 | async-start | bytes 1966080 | tf_op jit(solution)/shard_map/reduce_scatter | solution.py:36
  396.1 58.5 %reduce-scatter.25.cloned.1.call-start = ((), (), s32[]{:S(2)}) async-start(), calls=%async_computation.28 | async-start | bytes 1966080 | tf_op jit(solution)/shard_map/reduce_scatter | solution.py:36
  400.5 81.6 %all-gather.27.cloned.1.call-start = ((), (), s32[]{:S(2)}) async-start(), calls=%async_computation.29 | async-start | bytes 1966080 | tf_op jit(solution)/shard_map/all_gather | solution.py:32
  462.4 47.2 %all-gather.23.cloned.1.call-start = ((), (), s32[]{:S(2)}) async-start(), calls=%async_computation.25 | async-start | bytes 1966080 | tf_op jit(solution)/shard_map/all_gather | solution.py:32
  465.8 97.0 %reduce-scatter.27.cloned.1.call-start = ((), (), s32[]{:S(2)}) async-start(), calls=%async_computation.30 | async-start | bytes 1966080 | tf_op jit(solution)/shard_map/reduce_scatter | solution.py:36
  509.3 58.6 %reduce-scatter.23.cloned.1.call-start = ((), (), s32[]{:S(2)}) async-start(), calls=%async_computation.26 | async-start | bytes 1966080 | tf_op jit(solution)/shard_map/reduce_scatter | solution.py:36
  536.9 104.2 %reduce-scatter.35.cloned.1.call-start = ((), (), s32[]{:S(2)}) async-start(), calls=%async_computation.34 | async-start | bytes 1327104 | tf_op jit(solution)/shard_map/reduce_scatter | solution.py:42
  543.1 165.1 %reduce-scatter.33.cloned.1.call-start = ((), (), s32[]{:S(2)}) async-start(), calls=%async_computation.33 | async-start | bytes 1327104 | tf_op jit(solution)/shard_map/reduce_scatter | solution.py:42
  549.7 223.0 %reduce-scatter.31.cloned.1.call-start = ((), (), s32[]{:S(2)}) async-start(), calls=%async_computation.32 | async-start | bytes 442368 | tf_op jit(solution)/shard_map/reduce_scatter | solution.py:42
  557.2 281.9 %reduce-scatter.29.cloned.1.call-start = ((), (), s32[]{:S(2)}) async-start(), calls=%async_computation.31 | async-start | bytes 1105920 | tf_op jit(solution)/shard_map/reduce_scatter | solution.py:42
  568.9 145.5 %copy-start.28 = (bf16[3,64,1024]{2,1,0:T(8,128)(2,1)S(1)}, bf16[3,64,1024]{2,1,0:T(8,128)(2,1)}, u32[]{:S(2)}) copy-start(bf16[3,64,1024]{2,1,0:T(8,128)(2,1)} %copy-done.27) | copy-start | bytes 1179652
  568.9 145.5 %copy-start.30 = (bf16[3,64,1024]{2,1,0:T(8,128)(2,1)S(1)}, bf16[3,64,1024]{2,1,0:T(8,128)(2,1)}, u32[]{:S(2)}) copy-start(bf16[3,64,1024]{2,1,0:T(8,128)(2,1)} %copy-done.29) | copy-start | bytes 1179652
  571.8 268.9 %all-to-all-start.2 = ((bf16[256,2,768]{2,1,0:T(2,128)(2,1)}), bf16[256,2,768]{2,1,0:T(2,128)(2,1)S(1)}, u32[]{:S(2)}, u32[]{:S(2)}) async-start(bf16[256,2,768]{2,1,0:T(2,128)(2,1)} %copy.91), calls=%async_computation.10 | async-start | bytes 1572864 | tf_op jit(solution)/shard_map/all_to_all | solution.py:354
  714.4 127.1 %copy-start.57 = (s32[16]{0:T(128)S(1)}, s32[16]{0:T(128)}, u32[]{:S(2)}) copy-start(s32[16]{0:T(128)} %param.19) | copy-start | bytes 196
  714.4 128.4 %copy-start.1 = (bf16[32,16,768]{2,1,0:T(8,128)(2,1)S(1)}, bf16[32,16,768]{2,1,0:T(8,128)(2,1)}, u32[]{:S(2)}) copy-start(bf16[32,16,768]{2,1,0:T(8,128)(2,1)} %param.17) | copy-start | bytes 2359300
  (65 other events, 601.2 us)
Sparse Core Ops, SparseCore 0:
  39.1 18.6 all-gather.30
  59.9 19.6 all-gather.28
  123.8 27.3 reduce-scatter.12
  153.7 27.9 reduce-scatter.16
  340.0 19.6 all-gather.20
  361.1 19.6 all-gather.24
  462.5 19.6 all-gather.26
  483.7 19.6 all-gather.22
  509.4 27.9 reduce-scatter.26
  539.8 27.9 reduce-scatter.22
  571.2 69.7 reduce-scatter.34
  644.3 63.8 reduce-scatter.32
  711.5 61.2 reduce-scatter.30
  776.0 63.0 reduce-scatter.28
Sparse Core Ops, SparseCore 1:
  138.4 40.5 all-gather.14
  187.0 19.5 all-gather.18
  208.5 19.5 all-gather.12
  230.3 41.4 all-gather.16
  276.1 26.3 reduce-scatter.14
  305.0 27.9 reduce-scatter.18
  396.2 27.9 reduce-scatter.20
  426.6 27.9 reduce-scatter.24
where the time goes:
time: 859 us; the launch traced here: 850 us
  waiting for transfers between devices  452 us (53%)
  blocking collectives  153 us (18%)
  matrix products  136 us (16%)
  other arithmetic  55.4 us (6%)
  local copies, waits for them, and re-layouts  28.8 us (3%)
  between operations  16.9 us (2%)
    reduce_scatter x4, waiting for transfers between devices, scatter_weight(): lax.psum_scatter(grad.astype(jnp.bfloat16), 'dp', scatter_dimension=0, ti...  208 us
    reduce_scatter x8, waiting for transfers between devices, scatter_rows(): lax.psum_scatter(partial_sum.astype(jnp.bfloat16), 'tensor', scatter_dime...  131 us
    all_gather x8, waiting for transfers between devices, gather_rows(): return lax.all_gather(block, 'tensor', axis=0, tiled=True)  84.8 us
    unnamed x1, blocking collectives  40.2 us
    all_gather x1, blocking collectives, on_device(): project_full = lax.all_gather(project_weight, 'dp', axis=0, tiled=True)  32.5 us
    all_gather x1, blocking collectives, on_device(): lax.all_gather(attention_output_weight, 'dp', axis=0, tiled=True)  31.2 us
    all_to_all x1, blocking collectives, on_device(): lax.all_to_all(send_tokens, 'dp', split_axis=1, concat_axis=0, tiled=True)  27.4 us
    all_gather x1, waiting for transfers between devices, on_device(): down_full = lax.all_gather(feed_output_weight, 'dp', axis=0, tiled=True)  26.3 us
  transfers between devices with their start and end apart: 23, of which 16 were waited for; matrix products, arithmetic and copies ran while one was open for 18% of the time, Pallas kernels for 0%

commit v1 on v0

--- a/solution.py
+++ b/solution.py
@@ -98,8 +98,16 @@
         inner_rows // piece_rows * n_tensor + owner_rows
     ) * piece_rows + inner_rows % piece_rows
     key_valid = position[None, :] < seq_length[:, None]
-    project_full = lax.all_gather(project_weight, "dp", axis=0, tiled=True)
-    output_full = lax.all_gather(attention_output_weight, "dp", axis=0, tiled=True)
+    project_full, output_full = jnp.split(
+        lax.all_gather(
+            jnp.concatenate([project_weight, attention_output_weight], axis=1),
+            "dp",
+            axis=0,
+            tiled=True,
+        ),
+        [project_weight.shape[1]],
+        axis=1,
+    )
     up_full = lax.all_gather(feed_input_weight, "dp", axis=0, tiled=True)
     down_full = lax.all_gather(feed_output_weight, "dp", axis=0, tiled=True)
     query_part = lax.dynamic_slice_in_dim(

time: 859 us -> 890 us (1.036)
  waiting for transfers between devices: 452 us -> 546 us
  blocking collectives: 153 us -> 93.7 us
    all_gather x2 -> x0, blocking collectives: 63.7 us -> none  [the longest x1 32.5 us: on_device(): project_full = lax.all_gather(project_weight, 'dp', axis=0, tiled=True)]
    all_gather x8, waiting for transfers between devices: 84.8 us -> 128 us  [gather_rows(): return lax.all_gather(block, 'tensor', axis=0, tiled=True)]
    all_gather x1, waiting for transfers between devices: 0.01 us -> 35.5 us  [on_device(): up_full = lax.all_gather(feed_input_weight, 'dp', axis=0, tiled=True)]
    all_gather x0 -> x1, waiting for transfers between devices: none -> 11.9 us  [on_device(): lax.all_gather(jnp.concatenate([project_weight, attention_output_weight],...]
  transfers between devices with their start and end apart: 23 -> 24, of which waited for: 16 -> 20; matrix products, arithmetic and copies ran while one was open for 18% -> 18% of each run, Pallas kernels for 0% -> 0%
where the time goes in v1:
time: 890 us; the launch traced here: 882 us
  waiting for transfers between devices  546 us (61%)
  matrix products  136 us (15%)
  blocking collectives  93.7 us (11%)
  other arithmetic  56 us (6%)
  local copies, waits for them, and re-layouts  27.4 us (3%)
  between operations  15.5 us (2%)
    reduce_scatter x4, waiting for transfers between devices, scatter_weight(): lax.psum_scatter(grad.astype(jnp.bfloat16), 'dp', scatter_dimension=0, ti...  208 us
    reduce_scatter x8, waiting for transfers between devices, scatter_rows(): lax.psum_scatter(partial_sum.astype(jnp.bfloat16), 'tensor', scatter_dime...  134 us
    all_gather x8, waiting for transfers between devices, gather_rows(): return lax.all_gather(block, 'tensor', axis=0, tiled=True)  128 us
    unnamed x1, blocking collectives  40.1 us
    all_gather x1, waiting for transfers between devices, on_device(): up_full = lax.all_gather(feed_input_weight, 'dp', axis=0, tiled=True)  35.5 us
    all_to_all x1, blocking collectives, on_device(): lax.all_to_all(send_tokens, 'dp', split_axis=1, concat_axis=0, tiled=True)  32 us
    all_gather x1, waiting for transfers between devices, on_device(): down_full = lax.all_gather(feed_output_weight, 'dp', axis=0, tiled=True)  26 us
    dot_general x2, matrix products, on_device(): jnp.dot(first_full[s], up_full, preferred_element_type=jnp.float32)  22.2 us
  transfers between devices with their start and end apart: 24, of which 20 were waited for; matrix products, arithmetic and copies ran while one was open for 18% of the time, Pallas kernels for 0%

profile of v1, /device:TPU:0, one launch (start us, length us, event | category | flops | bytes accessed | tf_op | source)
XLA Modules:
  0.0 881.9 jit_solution(17437990461061641188)
XLA Ops:
  10.5 32.0 %all_to_all.54 = bf16[32,16,768]{2,0,1:T(8,128)(2,1)S(1)} all-to-all(bf16[32,16,768]{2,0,1:T(8,128)(2,1)S(1)} %copy.78), channel_id=1, replica_groups=mesh['dp'=8,'tensor'=4] {'dp'}, dimensions={1} | all-to-all | bytes 1572864 | tf_op jit(solution)/shard_map/all_to_all | solution.py:89
  46.2 11.9 %all-gather.14.cloned.1.call-done = bf16[768,768]{1,0:T(8,128)(2,1)} async-done(((bf16[96,768]{1,0:T(8,128)(2,1)}), bf16[768,768]{1,0:T(8,128)(2,1)}) %all-gather.14.cloned.1.call-update) | async-done | bytes 1179664 | tf_op jit(solution)/shard_map/all_gather | solution.py:102
  58.0 20.5 %all-gather.34.cloned.1.call-done = bf16[1024,1,768]{2,0,1:T(8,128)(2,1)} async-done(((bf16[256,1,768]{2,0,1:T(8,128)(2,1)}), bf16[1024,1,768]{2,0,1:T(8,128)(2,1)}) %all-gather.34.cloned.1.call-update) | async-done | bytes 1572880 | tf_op jit(solution)/shard_map/all_gather | solution.py:32
  81.4 18.9 %all-gather.32.cloned.1.call-done = bf16[1024,1,768]{2,0,1:T(8,128)(2,1)} async-done(((bf16[256,1,768]{2,0,1:T(8,128)(2,1)}), bf16[1024,1,768]{2,0,1:T(8,128)(2,1)}) %all-gather.32.cloned.1.call-update) | async-done | bytes 1572880 | tf_op jit(solution)/shard_map/all_gather | solution.py:32
  127.2 15.5 %reduce-scatter.13.cloned.1.call-done = bf16[256,768]{1,0:T(8,128)(2,1)} async-done(((bf16[1024,768]{1,0:T(8,128)(2,1)}), bf16[256,768]{1,0:T(8,128)(2,1)}) %reduce-scatter.13.cloned.1.call-update) | async-done | bytes 393232 | tf_op jit(solution)/shard_map/reduce_scatter | solution.py:36
  143.9 29.1 %reduce-scatter.17.cloned.1.call-done = bf16[256,768]{1,0:T(8,128)(2,1)} async-done(((bf16[1024,768]{1,0:T(8,128)(2,1)}), bf16[256,768]{1,0:T(8,128)(2,1)}) %reduce-scatter.17.cloned.1.call-update) | async-done | bytes 393232 | tf_op jit(solution)/shard_map/reduce_scatter | solution.py:36
  180.7 35.5 %all-gather.18.cloned.1.call-done = bf16[768,768]{1,0:T(8,128)(2,1)} async-done(((bf16[96,768]{1,0:T(8,128)(2,1)}), bf16[768,768]{1,0:T(8,128)(2,1)}) %all-gather.18.cloned.1.call-update) | async-done | bytes 1179664 | tf_op jit(solution)/shard_map/all_gather | solution.py:111
  216.3 20.5 %all-gather.22.cloned.1.call-done = bf16[1024,768]{1,0:T(8,128)(2,1)} async-done(((bf16[256,768]{1,0:T(8,128)(2,1)}), bf16[1024,768]{1,0:T(8,128)(2,1)}) %all-gather.22.cloned.1.call-update) | async-done | bytes 1572880 | tf_op jit(solution)/shard_map/all_gather | solution.py:32
  236.8 4.8 fusion.127
  241.6 17.0 %all-gather.16.cloned.1.call-done = bf16[1024,768]{1,0:T(8,128)(2,1)} async-done(((bf16[256,768]{1,0:T(8,128)(2,1)}), bf16[1024,768]{1,0:T(8,128)(2,1)}) %all-gather.16.cloned.1.call-update) | async-done | bytes 1572880 | tf_op jit(solution)/shard_map/all_gather | solution.py:32
  258.6 17.3 %multiply_convert_fusion.3 = (bf16[1024,768]{1,0:T(8,128)(2,1)}, f32[1024,768]{1,0:T(8,128)}, bf16[1024,768]{1,0:T(8,128)(2,1)}, f32[1024,768]{1,0:T(8,128)}, f32[1024,768]{1,0:T(8,128)}) fusion(f32[768]{0:T(1024)S(1)} %dynamic_slice.11, f32[1024,768]{1,0:T(8,128)} %fusion.127, bf16[1024,768]{1,0:T(8,128)(2,1)} %all-gather.16.cloned.1.call-done, ...), kind=kOutput, calls=%fused_computation.43 | convolution fusion | flops 1311768576 | bytes 18484224 | tf_op jit(solution)/shard_map/dot_general | solution.py:215
  275.9 26.0 %all-gather.20.cloned.1.call-done = bf16[768,768]{1,0:T(8,128)(2,1)} async-done(((bf16[96,768]{1,0:T(8,128)(2,1)}), bf16[768,768]{1,0:T(8,128)(2,1)}) %all-gather.20.cloned.1.call-update) | async-done | bytes 1179664 | tf_op jit(solution)/shard_map/all_gather | solution.py:112
  311.5 21.6 %all_to_all.55 = bf16[32,16,768]{2,0,1:T(8,128)(2,1)S(1)} all-to-all(bf16[32,16,768]{2,0,1:T(8,128)(2,1)S(1)} %copy.83), channel_id=1, replica_groups=mesh['dp'=8,'tensor'=4] {'dp'}, dimensions={1} | all-to-all | bytes 1572864 | tf_op jit(solution)/shard_map/all_to_all | solution.py:90
  333.3 30.5 %reduce-scatter.19.cloned.1.call-done = bf16[256,768]{1,0:T(8,128)(2,1)} async-done(((bf16[1024,768]{1,0:T(8,128)(2,1)}), bf16[256,768]{1,0:T(8,128)(2,1)}) %reduce-scatter.19.cloned.1.call-update) | async-done | bytes 393232 | tf_op jit(solution)/shard_map/reduce_scatter | solution.py:36
  371.8 18.7 %all-gather.24.cloned.1.call-done = bf16[1024,768]{1,0:T(8,128)(2,1)} async-done(((bf16[256,768]{1,0:T(8,128)(2,1)}), bf16[1024,768]{1,0:T(8,128)(2,1)}) %all-gather.24.cloned.1.call-update) | async-done | bytes 1572880 | tf_op jit(solution)/shard_map/all_gather | solution.py:32
  395.2 16.5 %all-gather.28.cloned.1.call-done = bf16[1024,768]{1,0:T(8,128)(2,1)} async-done(((bf16[256,768]{1,0:T(8,128)(2,1)}), bf16[1024,768]{1,0:T(8,128)(2,1)}) %all-gather.28.cloned.1.call-update) | async-done | bytes 1572880 | tf_op jit(solution)/shard_map/all_gather | solution.py:32
  411.7 11.5 %convert_reduce_fusion = (f32[768]{0:T(1024)}, bf16[1024,768]{1,0:T(8,128)(2,1)}, f32[768]{0:T(1024)}, bf16[1024,768]{1,0:T(8,128)(2,1)S(1)}) fusion(f32[1024,768]{1,0:T(8,128)} %get-tuple-element.152, f32[1024,768]{1,0:T(8,128)} %fusion.127, f32[768]{0:T(1024)} %copy-done.61, f32[1024,768]{1,0:T(8,128)} %fusion.128, f32[1024,768]{1,0:T(8,128)} %get-tuple-element.119, ...), kind=kOutput, calls=%fused_computation.26 | convolution fusion | flops 1234696704 | bytes 21636096 | tf_op jit(solution)/shard_map/dot_general | solution.py:240
  431.6 23.6 %reduce-scatter.21.cloned.1.call-done = bf16[256,768]{1,0:T(8,128)(2,1)} async-done(((bf16[1024,768]{1,0:T(8,128)(2,1)}), bf16[256,768]{1,0:T(8,128)(2,1)}) %reduce-scatter.21.cloned.1.call-update) | async-done | bytes 393232 | tf_op jit(solution)/shard_map/reduce_scatter | solution.py:36
  455.2 30.4 %reduce-scatter.25.cloned.1.call-done = bf16[256,768]{1,0:T(8,128)(2,1)} async-done(((bf16[1024,768]{1,0:T(8,128)(2,1)}), bf16[256,768]{1,0:T(8,128)(2,1)}) %reduce-scatter.25.cloned.1.call-update) | async-done | bytes 393232 | tf_op jit(solution)/shard_map/reduce_scatter | solution.py:36
  497.3 15.8 %all-gather.30.cloned.1.call-done = bf16[1024,768]{1,0:T(8,128)(2,1)} async-done(((bf16[256,768]{1,0:T(8,128)(2,1)}), bf16[1024,768]{1,0:T(8,128)(2,1)}) %all-gather.30.cloned.1.call-update) | async-done | bytes 1572880 | tf_op jit(solution)/shard_map/all_gather | solution.py:32
  515.5 6.1 multiply_reduce_fusion
  524.2 5.2 multiply_convert_fusion
  529.5 5.0 fusion.38
  543.7 6.5 multiply_reduce_fusion.1
  552.8 5.2 multiply_convert_fusion.1
  558.0 5.0 fusion.36
  603.9 5.5 all-to-all-start.2
  610.3 62.9 %reduce-scatter.35.cloned.1.call-done = bf16[96,768]{1,0:T(8,128)(2,1)} async-done(((bf16[768,768]{1,0:T(8,128)(2,1)}), bf16[96,768]{1,0:T(8,128)(2,1)}) %reduce-scatter.35.cloned.1.call-update) | async-done | bytes 147472 | tf_op jit(solution)/shard_map/reduce_scatter | solution.py:42
  674.8 65.5 %reduce-scatter.33.cloned.1.call-done = bf16[96,768]{1,0:T(8,128)(2,1)} async-done(((bf16[768,768]{1,0:T(8,128)(2,1)}), bf16[96,768]{1,0:T(8,128)(2,1)}) %reduce-scatter.33.cloned.1.call-update) | async-done | bytes 147472 | tf_op jit(solution)/shard_map/reduce_scatter | solution.py:42
  748.6 40.1 %all-reduce.2 = (f32[32,48]{1,0:T(8,128)S(1)}, f32[32,240]{1,0:T(8,128)S(1)}) all-reduce(f32[32,48]{1,0:T(8,128)S(1)} %pad_maximum_fusion.5, f32[32,240]{1,0:T(8,128)} %concatenate.25), channel_id=13, replica_groups=mesh['dp'=8,'tensor'=4] {'dp','tensor'}, use_global_device_ids=true, to_apply=%region_34.35.clone | all-reduce | flops 9216 | bytes 73728
  790.5 14.3 %reduce-scatter.31.cloned.1.call-done = bf16[96,192]{1,0:T(8,128)(2,1)} async-done(((bf16[768,192]{1,0:T(8,128)(2,1)}), bf16[96,192]{1,0:T(8,128)(2,1)}) %reduce-scatter.31.cloned.1.call-update) | async-done | bytes 36880 | tf_op jit(solution)/shard_map/reduce_scatter | solution.py:42
  806.2 65.1 %reduce-scatter.29.cloned.1.call-done = bf16[96,576]{1,0:T(8,128)(2,1)} async-done(((bf16[768,576]{1,0:T(8,128)(2,1)}), bf16[96,576]{1,0:T(8,128)(2,1)}) %reduce-scatter.29.cloned.1.call-update) | async-done | bytes 110608 | tf_op jit(solution)/shard_map/reduce_scatter | solution.py:42
  (335 shorter events, 162.2 us)
Async XLA Ops:
  7.2 50.8 %all-gather.14.cloned.1.call-start = ((), (), s32[]{:S(2)}) async-start(), calls=%async_computation.15 | async-start | bytes 1327104 | tf_op jit(solution)/shard_map/all_gather | solution.py:102
  9.0 69.5 %all-gather.34.cloned.1.call-start = ((), (), s32[]{:S(2)}) async-start(), calls=%async_computation.37 | async-start | bytes 1966080 | tf_op jit(solution)/shard_map/all_gather | solution.py:32
  43.5 56.9 %all-gather.32.cloned.1.call-start = ((), (), s32[]{:S(2)}) async-start(), calls=%async_computation.36 | async-start | bytes 1966080 | tf_op jit(solution)/shard_map/all_gather | solution.py:32
  44.2 98.4 %reduce-scatter.13.cloned.1.call-start = ((), (), s32[]{:S(2)}) async-start(), calls=%async_computation.16 | async-start | bytes 1966080 | tf_op jit(solution)/shard_map/reduce_scatter | solution.py:36
  114.5 58.6 %reduce-scatter.17.cloned.1.call-start = ((), (), s32[]{:S(2)}) async-start(), calls=%async_computation.21 | async-start | bytes 1966080 | tf_op jit(solution)/shard_map/reduce_scatter | solution.py:36
  126.6 89.7 %all-gather.18.cloned.1.call-start = ((), (), s32[]{:S(2)}) async-start(), calls=%async_computation.18 | async-start | bytes 1327104 | tf_op jit(solution)/shard_map/all_gather | solution.py:111
  127.1 109.6 %all-gather.22.cloned.1.call-start = ((), (), s32[]{:S(2)}) async-start(), calls=%async_computation.22 | async-start | bytes 1966080 | tf_op jit(solution)/shard_map/all_gather | solution.py:32
  174.6 189.2 %copy-start.52 = (f32[256]{0:T(256)}, f32[256]{0:T(256)S(1)}, u32[]{:S(2)}) copy-start(f32[256]{0:T(256)S(1)} %get-tuple-element.164) | copy-start | bytes 3076
  175.9 187.9 %copy-start.51 = (f32[256]{0:T(256)}, f32[256]{0:T(256)S(1)}, u32[]{:S(2)}) copy-start(f32[256]{0:T(256)S(1)} %add_rsqrt_fusion.1) | copy-start | bytes 3076
  178.3 80.3 %all-gather.16.cloned.1.call-start = ((), (), s32[]{:S(2)}) async-start(), calls=%async_computation.17 | async-start | bytes 1966080 | tf_op jit(solution)/shard_map/all_gather | solution.py:32
  179.0 122.9 %all-gather.20.cloned.1.call-start = ((), (), s32[]{:S(2)}) async-start(), calls=%async_computation.19 | async-start | bytes 1327104 | tf_op jit(solution)/shard_map/all_gather | solution.py:112
  179.7 153.5 %reduce-scatter.15.cloned.1.call-start = ((), (), s32[]{:S(2)}) async-start(), calls=%async_computation.20 | async-start | bytes 1966080 | tf_op jit(solution)/shard_map/reduce_scatter | solution.py:36
  180.7 77.8 %copy-start.61 = (f32[768]{0:T(1024)}, f32[768]{0:T(1024)S(1)}, u32[]{:S(2)}) copy-start(f32[768]{0:T(1024)S(1)} %dynamic_slice.11) | copy-start | bytes 9220
  306.2 57.5 %reduce-scatter.19.cloned.1.call-start = ((), (), s32[]{:S(2)}) async-start(), calls=%async_computation.23 | async-start | bytes 1966080 | tf_op jit(solution)/shard_map/reduce_scatter | solution.py:36
  310.7 53.1 %copy-start.7 = (bf16[256,768]{1,0:T(8,128)(2,1)S(1)}, bf16[256,768]{1,0:T(8,128)(2,1)}, u32[]{:S(2)}) copy-start(bf16[256,768]{1,0:T(8,128)(2,1)} %reduce-scatter.17.cloned.1.call-done) | copy-start | bytes 1179652
  310.7 53.1 %copy-start.56 = (f32[768]{0:T(1024)S(1)}, f32[768]{0:T(1024)}, u32[]{:S(2)}) copy-start(f32[768]{0:T(1024)} %param.26) | copy-start | bytes 9220
  310.7 79.7 %all-gather.24.cloned.1.call-start = ((), (), s32[]{:S(2)}) async-start(), calls=%async_computation.24 | async-start | bytes 1966080 | tf_op jit(solution)/shard_map/all_gather | solution.py:32
  370.7 41.0 %all-gather.28.cloned.1.call-start = ((), (), s32[]{:S(2)}) async-start(), calls=%async_computation.28 | async-start | bytes 1966080 | tf_op jit(solution)/shard_map/all_gather | solution.py:32
  371.6 83.6 %reduce-scatter.21.cloned.1.call-start = ((), (), s32[]{:S(2)}) async-start(), calls=%async_computation.25 | async-start | bytes 1966080 | tf_op jit(solution)/shard_map/reduce_scatter | solution.py:36
  427.1 58.6 %reduce-scatter.25.cloned.1.call-start = ((), (), s32[]{:S(2)}) async-start(), calls=%async_computation.29 | async-start | bytes 1966080 | tf_op jit(solution)/shard_map/reduce_scatter | solution.py:36
  431.5 81.6 %all-gather.30.cloned.1.call-start = ((), (), s32[]{:S(2)}) async-start(), calls=%async_computation.30 | async-start | bytes 1966080 | tf_op jit(solution)/shard_map/all_gather | solution.py:32
  493.4 48.1 %all-gather.26.cloned.1.call-start = ((), (), s32[]{:S(2)}) async-start(), calls=%async_computation.26 | async-start | bytes 1966080 | tf_op jit(solution)/shard_map/all_gather | solution.py:32
  496.9 96.8 %reduce-scatter.27.cloned.1.call-start = ((), (), s32[]{:S(2)}) async-start(), calls=%async_computation.31 | async-start | bytes 1966080 | tf_op jit(solution)/shard_map/reduce_scatter | solution.py:36
  541.3 58.7 %reduce-scatter.23.cloned.1.call-start = ((), (), s32[]{:S(2)}) async-start(), calls=%async_computation.27 | async-start | bytes 1966080 | tf_op jit(solution)/shard_map/reduce_scatter | solution.py:36
  569.0 104.2 %reduce-scatter.35.cloned.1.call-start = ((), (), s32[]{:S(2)}) async-start(), calls=%async_computation.35 | async-start | bytes 1327104 | tf_op jit(solution)/shard_map/reduce_scatter | solution.py:42
  575.2 165.2 %reduce-scatter.33.cloned.1.call-start = ((), (), s32[]{:S(2)}) async-start(), calls=%async_computation.34 | async-start | bytes 1327104 | tf_op jit(solution)/shard_map/reduce_scatter | solution.py:42
  581.7 223.1 %reduce-scatter.31.cloned.1.call-start = ((), (), s32[]{:S(2)}) async-start(), calls=%async_computation.33 | async-start | bytes 442368 | tf_op jit(solution)/shard_map/reduce_scatter | solution.py:42
  588.1 283.3 %reduce-scatter.29.cloned.1.call-start = ((), (), s32[]{:S(2)}) async-start(), calls=%async_computation.32 | async-start | bytes 1105920 | tf_op jit(solution)/shard_map/reduce_scatter | solution.py:42
  601.1 145.5 %copy-start.36 = (bf16[3,64,1024]{2,1,0:T(8,128)(2,1)S(1)}, bf16[3,64,1024]{2,1,0:T(8,128)(2,1)}, u32[]{:S(2)}) copy-start(bf16[3,64,1024]{2,1,0:T(8,128)(2,1)} %copy-done.35) | copy-start | bytes 1179652
  603.9 269.1 %all-to-all-start.2 = ((bf16[256,2,768]{2,1,0:T(2,128)(2,1)}), bf16[256,2,768]{2,1,0:T(2,128)(2,1)S(1)}, u32[]{:S(2)}, u32[]{:S(2)}) async-start(bf16[256,2,768]{2,1,0:T(2,128)(2,1)} %copy.91), calls=%async_computation.10 | async-start | bytes 1572864 | tf_op jit(solution)/shard_map/all_to_all | solution.py:362
  746.5 127.3 %copy-start.60 = (s32[16]{0:T(128)S(1)}, s32[16]{0:T(128)}, u32[]{:S(2)}) copy-start(s32[16]{0:T(128)} %param.19) | copy-start | bytes 196
  746.5 128.6 %copy-start.1 = (bf16[32,16,768]{2,1,0:T(8,128)(2,1)S(1)}, bf16[32,16,768]{2,1,0:T(8,128)(2,1)}, u32[]{:S(2)}) copy-start(bf16[32,16,768]{2,1,0:T(8,128)(2,1)} %param.17) | copy-start | bytes 2359300
  (70 other events, 755.3 us)
Sparse Core Ops, SparseCore 0:
  10.8 47.2 all-gather.13
  60.2 18.3 all-gather.33
  80.7 19.6 all-gather.31
  114.6 28.0 reduce-scatter.12
  145.0 28.0 reduce-scatter.16
  175.1 41.1 all-gather.17
  218.4 18.3 all-gather.21
  238.9 19.6 all-gather.15
  260.7 41.1 all-gather.19
  306.4 26.7 reduce-scatter.14
  335.7 28.0 reduce-scatter.18
  370.8 19.6 all-gather.23
  392.0 19.6 all-gather.27
  427.2 27.9 reduce-scatter.20
  457.6 27.9 reduce-scatter.24
  493.5 19.6 all-gather.29
  514.6 19.6 all-gather.25
  541.4 28.0 reduce-scatter.26
  572.0 27.9 reduce-scatter.22
  603.2 69.8 reduce-scatter.34
  676.6 63.7 reduce-scatter.32
  743.6 61.1 reduce-scatter.30
  808.2 63.1 reduce-scatter.28
